TPU v7x, 32 devices: a whole 2x2x4 slice. The times are simulated.
32 devices in a mesh: parts: 2 (over y), pix: 4 (over z), par: 4 (over x, core).
Axes of the slice: x: 2, y: 2, z: 4, core: 2. Of those that a mesh axis runs over, the one named last changes fastest.
Arguments:
- green_matrix: bfloat16 [4608, 16384], P('pix', 'par'), may hold values from -0.046875 to 0.046875
- observed: bfloat16 [64, 4608], P('parts', 'pix'), parts along dimension 0, may hold values from -1000 to 1000
Outputs:
- solution: float32 [64, 16384], P('parts', 'par'), parts along dimension 0
- residual: float32 [64, 4608], P('parts', 'pix'), parts along dimension 0
There are 2 independent parts, one for each index of `parts`. A program takes and returns all parts, laid end to end along the dimension named above; an argument that names none is the same for every part. Nothing has to cross between parts.
All inputs are finite; a program needn't handle non-finite values.
Results may differ from a plain program's by a relative error of at most 0.0038.
Values may be sent and summed in bfloat16 or wider, within the bound.
No kernel may reach another device: no remote copies, remote signals or barrier semaphores. Data moves between devices by JAX's collectives and lax.ppermute only.
A program may use at most 64 MiB of HBM per device.

v0:
```python
import jax
import jax.numpy as jnp
from jax import lax
from jax.sharding import PartitionSpec as P

GRID = 128
ITERS = 5


def padded_2(block, sides, width):
    for axis, dim in sides:
        count = lax.axis_size(axis)
        forward = [(i, i + 1) for i in range(count - 1)]
        backward = [(target, source) for source, target in forward]
        low = lax.ppermute(
            lax.slice_in_dim(block, block.shape[dim] - width, None, axis=dim), axis, forward
        )
        high = lax.ppermute(lax.slice_in_dim(block, 0, width, axis=dim), axis, backward)
        block = jnp.concatenate([low, block, high], axis=dim)
    return block


def smooth(values):
    set_count = values.shape[0]
    grid_rows = values.shape[1] // GRID
    tiles = values.reshape(set_count, grid_rows, GRID)
    padded = padded_2(tiles, (("par", 1),), 1)
    padded = jnp.pad(padded, ((0, 0), (0, 0), (1, 1)))
    beside_all = (
        padded[:, 2:, 1:-1] + padded[:, :-2, 1:-1] + padded[:, 1:-1, 2:] + padded[:, 1:-1, :-2]
    )
    return (0.25 * (4.0 * tiles - beside_all)).reshape(set_count, grid_rows * GRID)


def forward(rounded, green_matrix):
    partial_value = lax.dot_general(
        rounded, green_matrix, (((1,), (1,)), ((), ())), preferred_element_type=jnp.float32
    )
    return lax.psum(partial_value, "par")


def curvatures(image, smoothed):
    local_image = jnp.sum(image * image, axis=1)
    local_smooth = jnp.sum(smoothed * smoothed, axis=1)
    image_sq = lax.psum(local_image, "pix")
    smooth_sq = lax.psum(local_smooth, "par")
    return image_sq + smooth_sq


def backward_sum(rounded, green_matrix):
    return lax.psum(jnp.dot(rounded, green_matrix, preferred_element_type=jnp.float32), "pix")


def column_squares(gradient):
    return lax.psum(jnp.sum(gradient * gradient, axis=1), "par")


def on_device(green_matrix, observed):
    set_count = observed.shape[0]
    tile_cells = green_matrix.shape[1]
    residual = observed.astype(jnp.float32)
    gradient = backward_sum(observed, green_matrix)
    grad_sq = column_squares(gradient)
    direction = gradient
    solution = jnp.zeros((set_count, tile_cells), jnp.float32)
    smooth_res = jnp.zeros((set_count, tile_cells), jnp.float32)
    for sweep in range(ITERS):
        rounded = direction.astype(jnp.bfloat16)
        image = forward(rounded, green_matrix)
        smoothed = smooth(lax.optimization_barrier(rounded).astype(jnp.float32))
        step_len = (grad_sq / curvatures(image, smoothed))[:, None]
        solution = solution + step_len * direction
        residual = residual - step_len * image
        smooth_res = smooth_res - step_len * smoothed
        if sweep + 1 < ITERS:
            gradient = backward_sum(residual.astype(jnp.bfloat16), green_matrix) + smooth(
                smooth_res
            )
            fresh_sq = column_squares(gradient)
            direction = gradient + (fresh_sq / grad_sq)[:, None] * direction
            grad_sq = fresh_sq
    return (solution, residual)


def solution(mesh):
    return jax.shard_map(
        on_device,
        mesh=mesh,
        in_specs=(P("pix", "par"), P("parts", "pix")),
        out_specs=(P("parts", "par"), P("parts", "pix")),
        check_vma=False,
    )
```

profile of v0, /device:TPU:0, one launch (start us, length us, event | category | flops | bytes accessed | tf_op | source)
XLA Modules:
  0.0 557.3 jit_solution(6629463593647099205)
XLA Ops:
  13.5 41.3 %all-reduce.21.cloned.1.call-done = f32[32,4096]{1,0:T(8,128)} async-done(((f32[32,4096]{1,0:T(8,128)}), f32[32,4096]{1,0:T(8,128)}) %all-reduce.21.cloned.1.call-update) | async-done | bytes 524304 | tf_op jit(solution)/shard_map/psum | solution.py:51
  59.0 7.2 %fusion.54 = f32[32,1152]{1,0:T(8,128)} fusion(bf16[32,4096]{1,0:T(8,128)(2,1)S(1)} %get-tuple-element.45, bf16[1152,4096]{1,0:T(8,128)(2,1)} %param.2), kind=kOutput, calls=%fused_computation.151 | convolution fusion | flops 301989888 | bytes 9846784 | tf_op jit(solution)/shard_map/dot_general | solution.py:36
  67.5 8.5 %all-reduce.9 = (f32[32]{0:T(128)S(1)}, f32[32]{0:T(128)S(1)}) all-reduce(f32[32]{0:T(128)S(1)} %get-tuple-element.44, f32[32]{0:T(128)S(1)} %get-tuple-element.24), channel_id=1, replica_groups=mesh['parts'=2,'pix'=4,'par'=4] {'par'}, use_global_device_ids=true, to_apply=%region_2.0 | all-reduce | flops 64 | bytes 512 | tf_op jit(solution)/shard_map/psum | solution.py:55
  75.9 24.4 %all-reduce.23.cloned.1.call-done = f32[32,1152]{1,0:T(8,128)} async-done(((f32[32,1152]{1,0:T(8,128)}), f32[32,1152]{1,0:T(8,128)}) %all-reduce.23.cloned.1.call-update) | async-done | bytes 147472 | tf_op jit(solution)/shard_map/psum | solution.py:39
  101.3 11.7 %psum.178 = f32[32]{0:T(128)S(1)} all-reduce(f32[32]{0:T(128)S(1)} %multiply_reduce_fusion.13), channel_id=1, replica_groups=mesh['parts'=2,'pix'=4,'par'=4] {'pix'}, use_global_device_ids=true, to_apply=%region_5.6 | all-reduce | flops 32 | bytes 256 | tf_op jit(solution)/shard_map/psum | solution.py:45
  126.5 29.6 %all-reduce.25.cloned.1.call-done = f32[32,4096]{1,0:T(8,128)} async-done(((f32[32,4096]{1,0:T(8,128)}), f32[32,4096]{1,0:T(8,128)}) %all-reduce.25.cloned.1.call-update) | async-done | bytes 524304 | tf_op jit(solution)/shard_map/psum | solution.py:51
  166.9 7.2 %fusion.55 = f32[32,1152]{1,0:T(8,128)} fusion(bf16[32,4096]{1,0:T(8,128)(2,1)S(1)} %get-tuple-element.20, bf16[1152,4096]{1,0:T(8,128)(2,1)} %param.2), kind=kOutput, calls=%fused_computation.152 | convolution fusion | flops 301989888 | bytes 9846784 | tf_op jit(solution)/shard_map/dot_general | solution.py:36
  175.4 8.4 %psum.184 = f32[32]{0:T(128)S(1)} all-reduce(f32[32]{0:T(128)S(1)} %get-tuple-element.18), channel_id=1, replica_groups=mesh['parts'=2,'pix'=4,'par'=4] {'par'}, use_global_device_ids=true, to_apply=%region_15.16 | all-reduce | flops 32 | bytes 256 | tf_op jit(solution)/shard_map/psum | solution.py:46
  183.8 24.2 %all-reduce.27.cloned.1.call-done = f32[32,1152]{1,0:T(8,128)} async-done(((f32[32,1152]{1,0:T(8,128)}), f32[32,1152]{1,0:T(8,128)}) %all-reduce.27.cloned.1.call-update) | async-done | bytes 147472 | tf_op jit(solution)/shard_map/psum | solution.py:39
  209.0 11.7 %psum.183 = f32[32]{0:T(128)S(1)} all-reduce(f32[32]{0:T(128)S(1)} %multiply_reduce_fusion.12), channel_id=1, replica_groups=mesh['parts'=2,'pix'=4,'par'=4] {'pix'}, use_global_device_ids=true, to_apply=%region_13.14 | all-reduce | flops 32 | bytes 256 | tf_op jit(solution)/shard_map/psum | solution.py:45
  235.0 29.6 %all-reduce.29.cloned.1.call-done = f32[32,4096]{1,0:T(8,128)} async-done(((f32[32,4096]{1,0:T(8,128)}), f32[32,4096]{1,0:T(8,128)}) %all-reduce.29.cloned.1.call-update) | async-done | bytes 524304 | tf_op jit(solution)/shard_map/psum | solution.py:51
  275.4 7.2 %fusion.56 = f32[32,1152]{1,0:T(8,128)} fusion(bf16[32,4096]{1,0:T(8,128)(2,1)S(1)} %get-tuple-element.14, bf16[1152,4096]{1,0:T(8,128)(2,1)} %param.2), kind=kOutput, calls=%fused_computation.153 | convolution fusion | flops 301989888 | bytes 9846784 | tf_op jit(solution)/shard_map/dot_general | solution.py:36
  283.9 8.3 %psum.189 = f32[32]{0:T(128)S(1)} all-reduce(f32[32]{0:T(128)S(1)} %get-tuple-element.12), channel_id=1, replica_groups=mesh['parts'=2,'pix'=4,'par'=4] {'par'}, use_global_device_ids=true, to_apply=%region_23.24 | all-reduce | flops 32 | bytes 256 | tf_op jit(solution)/shard_map/psum | solution.py:46
  292.1 24.4 %all-reduce.31.cloned.1.call-done = f32[32,1152]{1,0:T(8,128)} async-done(((f32[32,1152]{1,0:T(8,128)}), f32[32,1152]{1,0:T(8,128)}) %all-reduce.31.cloned.1.call-update) | async-done | bytes 147472 | tf_op jit(solution)/shard_map/psum | solution.py:39
  317.5 11.7 %psum.188 = f32[32]{0:T(128)S(1)} all-reduce(f32[32]{0:T(128)S(1)} %multiply_reduce_fusion.11), channel_id=1, replica_groups=mesh['parts'=2,'pix'=4,'par'=4] {'pix'}, use_global_device_ids=true, to_apply=%region_21.22 | all-reduce | flops 32 | bytes 256 | tf_op jit(solution)/shard_map/psum | solution.py:45
  342.7 29.6 %all-reduce.33.cloned.1.call-done = f32[32,4096]{1,0:T(8,128)} async-done(((f32[32,4096]{1,0:T(8,128)}), f32[32,4096]{1,0:T(8,128)}) %all-reduce.33.cloned.1.call-update) | async-done | bytes 524304 | tf_op jit(solution)/shard_map/psum | solution.py:51
  393.4 8.3 %psum.194 = f32[32]{0:T(128)S(1)} all-reduce(f32[32]{0:T(128)S(1)} %get-tuple-element.6), channel_id=1, replica_groups=mesh['parts'=2,'pix'=4,'par'=4] {'par'}, use_global_device_ids=true, to_apply=%region_31.32 | all-reduce | flops 32 | bytes 256 | tf_op jit(solution)/shard_map/psum | solution.py:46
  401.7 23.6 %all-reduce.35.cloned.1.call-done = f32[32,1152]{1,0:T(8,128)} async-done(((f32[32,1152]{1,0:T(8,128)}), f32[32,1152]{1,0:T(8,128)}) %all-reduce.35.cloned.1.call-update) | async-done | bytes 147472 | tf_op jit(solution)/shard_map/psum | solution.py:39
  426.4 11.7 %psum.193 = f32[32]{0:T(128)S(1)} all-reduce(f32[32]{0:T(128)S(1)} %multiply_reduce_fusion.10), channel_id=1, replica_groups=mesh['parts'=2,'pix'=4,'par'=4] {'pix'}, use_global_device_ids=true, to_apply=%region_29.30 | all-reduce | flops 32 | bytes 256 | tf_op jit(solution)/shard_map/psum | solution.py:45
  453.1 29.6 %all-reduce.37.cloned.1.call-done = f32[32,4096]{1,0:T(8,128)} async-done(((f32[32,4096]{1,0:T(8,128)}), f32[32,4096]{1,0:T(8,128)}) %all-reduce.37.cloned.1.call-update) | async-done | bytes 524304 | tf_op jit(solution)/shard_map/psum | solution.py:51
  493.5 7.2 %fusion.58 = f32[32,1152]{1,0:T(8,128)} fusion(bf16[32,4096]{1,0:T(8,128)(2,1)S(1)} %fusion.26, bf16[1152,4096]{1,0:T(8,128)(2,1)} %param.2), kind=kOutput, calls=%fused_computation.155 | convolution fusion | flops 301989888 | bytes 9846784 | tf_op jit(solution)/shard_map/dot_general | solution.py:36
  501.9 8.3 %psum.199 = f32[32]{0:T(128)S(1)} all-reduce(f32[32]{0:T(128)S(1)} %fusion.4), channel_id=1, replica_groups=mesh['parts'=2,'pix'=4,'par'=4] {'par'}, use_global_device_ids=true, to_apply=%region_39.40 | all-reduce | flops 32 | bytes 256 | tf_op jit(solution)/shard_map/psum | solution.py:46
  510.2 24.4 %all-reduce.39.cloned.1.call-done = f32[32,1152]{1,0:T(8,128)} async-done(((f32[32,1152]{1,0:T(8,128)}), f32[32,1152]{1,0:T(8,128)}) %all-reduce.39.cloned.1.call-update) | async-done | bytes 147472 | tf_op jit(solution)/shard_map/psum | solution.py:39
  535.6 11.7 %psum.198 = f32[32]{0:T(128)S(1)} all-reduce(f32[32]{0:T(128)S(1)} %multiply_reduce_fusion.9), channel_id=1, replica_groups=mesh['parts'=2,'pix'=4,'par'=4] {'pix'}, use_global_device_ids=true, to_apply=%region_37.38 | all-reduce | flops 32 | bytes 256 | tf_op jit(solution)/shard_map/psum | solution.py:45
  (156 shorter events, 132.7 us)
Async XLA Ops:
  7.2 47.7 %all-reduce.21.cloned.1.call-start = ((), (), s32[]{:S(2)}) async-start(), calls=%async_computation | async-start | bytes 1048576 | tf_op jit(solution)/shard_map/psum | solution.py:51
  13.5 86.8 %all-reduce.23.cloned.1.call-start = ((), (), s32[]{:S(2)}) async-start(), calls=%async_computation.1 | async-start | bytes 294912 | tf_op jit(solution)/shard_map/psum | solution.py:39
  56.4 9.9 %collective-permute-start.1 = (f32[32,1,128]{2,1,0:T(1,128)S(1)}, f32[32,1,128]{2,1,0:T(1,128)S(1)}, u32[]{:S(2)}, u32[]{:S(2)}) collective-permute-start(f32[32,1,128]{2,1,0:T(1,128)S(1)} %get-tuple-element.42), channel_id=1, source_target_pairs={{0,1},{1,2},{2,3},{4,5},{5,6},{6,7},{8,9},{9,10},{10,11},{12,13},{... | collective-permute-start | bytes 49160 | tf_op jit(solution)/shard_map/ppermute | solution.py:15
  57.7 8.6 %collective-permute-start = (f32[32,1,128]{2,1,0:T(1,128)S(1)}, f32[32,1,128]{2,1,0:T(1,128)S(1)}, u32[]{:S(2)}, u32[]{:S(2)}) collective-permute-start(f32[32,1,128]{2,1,0:T(1,128)S(1)} %get-tuple-element.43), channel_id=1, source_target_pairs={{1,0},{2,1},{3,2},{5,4},{6,5},{7,6},{9,8},{10,9},{11,10},{13,12},{... | collective-permute-start | bytes 49160 | tf_op jit(solution)/shard_map/ppermute | solution.py:18
  66.3 89.8 %all-reduce.25.cloned.1.call-start = ((), (), s32[]{:S(2)}) async-start(), calls=%async_computation.2 | async-start | bytes 1048576 | tf_op jit(solution)/shard_map/psum | solution.py:51
  119.4 88.6 %all-reduce.27.cloned.1.call-start = ((), (), s32[]{:S(2)}) async-start(), calls=%async_computation.3 | async-start | bytes 294912 | tf_op jit(solution)/shard_map/psum | solution.py:39
  120.9 4.6 collective-permute-start.2
  163.8 10.4 %collective-permute-start.5 = (f32[32,1,128]{2,1,0:T(1,128)S(1)}, f32[32,1,128]{2,1,0:T(1,128)S(1)}, u32[]{:S(2)}, u32[]{:S(2)}) collective-permute-start(f32[32,1,128]{2,1,0:T(1,128)S(1)} %get-tuple-element.38), channel_id=1, source_target_pairs={{0,1},{1,2},{2,3},{4,5},{5,6},{6,7},{8,9},{9,10},{10,11},{12,13},{... | collective-permute-start | bytes 49160 | tf_op jit(solution)/shard_map/ppermute | solution.py:15
  165.6 8.6 %collective-permute-start.4 = (f32[32,1,128]{2,1,0:T(1,128)S(1)}, f32[32,1,128]{2,1,0:T(1,128)S(1)}, u32[]{:S(2)}, u32[]{:S(2)}) collective-permute-start(f32[32,1,128]{2,1,0:T(1,128)S(1)} %get-tuple-element.39), channel_id=1, source_target_pairs={{1,0},{2,1},{3,2},{5,4},{6,5},{7,6},{9,8},{10,9},{11,10},{13,12},{... | collective-permute-start | bytes 49160 | tf_op jit(solution)/shard_map/ppermute | solution.py:18
  174.2 90.4 %all-reduce.29.cloned.1.call-start = ((), (), s32[]{:S(2)}) async-start(), calls=%async_computation.4 | async-start | bytes 1048576 | tf_op jit(solution)/shard_map/psum | solution.py:51
  228.0 88.5 %all-reduce.31.cloned.1.call-start = ((), (), s32[]{:S(2)}) async-start(), calls=%async_computation.5 | async-start | bytes 294912 | tf_op jit(solution)/shard_map/psum | solution.py:39
  229.5 4.6 collective-permute-start.6
  272.4 10.4 %collective-permute-start.9 = (f32[32,1,128]{2,1,0:T(1,128)S(1)}, f32[32,1,128]{2,1,0:T(1,128)S(1)}, u32[]{:S(2)}, u32[]{:S(2)}) collective-permute-start(f32[32,1,128]{2,1,0:T(1,128)S(1)} %get-tuple-element.34), channel_id=1, source_target_pairs={{0,1},{1,2},{2,3},{4,5},{5,6},{6,7},{8,9},{9,10},{10,11},{12,13},{... | collective-permute-start | bytes 49160 | tf_op jit(solution)/shard_map/ppermute | solution.py:15
  274.1 8.6 %collective-permute-start.8 = (f32[32,1,128]{2,1,0:T(1,128)S(1)}, f32[32,1,128]{2,1,0:T(1,128)S(1)}, u32[]{:S(2)}, u32[]{:S(2)}) collective-permute-start(f32[32,1,128]{2,1,0:T(1,128)S(1)} %get-tuple-element.35), channel_id=1, source_target_pairs={{1,0},{2,1},{3,2},{5,4},{6,5},{7,6},{9,8},{10,9},{11,10},{13,12},{... | collective-permute-start | bytes 49160 | tf_op jit(solution)/shard_map/ppermute | solution.py:18
  282.7 89.6 %all-reduce.33.cloned.1.call-start = ((), (), s32[]{:S(2)}) async-start(), calls=%async_computation.6 | async-start | bytes 1048576 | tf_op jit(solution)/shard_map/psum | solution.py:51
  335.6 89.7 %all-reduce.35.cloned.1.call-start = ((), (), s32[]{:S(2)}) async-start(), calls=%async_computation.7 | async-start | bytes 294912 | tf_op jit(solution)/shard_map/psum | solution.py:39
  337.1 4.6 collective-permute-start.10
  381.0 10.6 %collective-permute-start.13 = (f32[32,1,128]{2,1,0:T(1,128)S(1)}, f32[32,1,128]{2,1,0:T(1,128)S(1)}, u32[]{:S(2)}, u32[]{:S(2)}) collective-permute-start(f32[32,1,128]{2,1,0:T(1,128)S(1)} %get-tuple-element.30), channel_id=1, source_target_pairs={{0,1},{1,2},{2,3},{4,5},{5,6},{6,7},{8,9},{9,10},{10,11},{12,13},{... | collective-permute-start | bytes 49160 | tf_op jit(solution)/shard_map/ppermute | solution.py:15
  382.8 8.8 %collective-permute-start.12 = (f32[32,1,128]{2,1,0:T(1,128)S(1)}, f32[32,1,128]{2,1,0:T(1,128)S(1)}, u32[]{:S(2)}, u32[]{:S(2)}) collective-permute-start(f32[32,1,128]{2,1,0:T(1,128)S(1)} %get-tuple-element.31), channel_id=1, source_target_pairs={{1,0},{2,1},{3,2},{5,4},{6,5},{7,6},{9,8},{10,9},{11,10},{13,12},{... | collective-permute-start | bytes 49160 | tf_op jit(solution)/shard_map/ppermute | solution.py:18
  391.5 91.2 %all-reduce.37.cloned.1.call-start = ((), (), s32[]{:S(2)}) async-start(), calls=%async_computation.8 | async-start | bytes 1048576 | tf_op jit(solution)/shard_map/psum | solution.py:51
  446.1 88.5 %all-reduce.39.cloned.1.call-start = ((), (), s32[]{:S(2)}) async-start(), calls=%async_computation.9 | async-start | bytes 294912 | tf_op jit(solution)/shard_map/psum | solution.py:39
  447.6 4.6 collective-permute-start.14
  490.5 10.3 %collective-permute-start.17 = (f32[32,1,128]{2,1,0:T(1,128)S(1)}, f32[32,1,128]{2,1,0:T(1,128)S(1)}, u32[]{:S(2)}, u32[]{:S(2)}) collective-permute-start(f32[32,1,128]{2,1,0:T(1,128)S(1)} %get-tuple-element.26), channel_id=1, source_target_pairs={{0,1},{1,2},{2,3},{4,5},{5,6},{6,7},{8,9},{9,10},{10,11},{12,13},{... | collective-permute-start | bytes 49160 | tf_op jit(solution)/shard_map/ppermute | solution.py:15
  492.2 8.6 %collective-permute-start.16 = (f32[32,1,128]{2,1,0:T(1,128)S(1)}, f32[32,1,128]{2,1,0:T(1,128)S(1)}, u32[]{:S(2)}, u32[]{:S(2)}) collective-permute-start(f32[32,1,128]{2,1,0:T(1,128)S(1)} %get-tuple-element.27), channel_id=1, source_target_pairs={{1,0},{2,1},{3,2},{5,4},{6,5},{7,6},{9,8},{10,9},{11,10},{13,12},{... | collective-permute-start | bytes 49160 | tf_op jit(solution)/shard_map/ppermute | solution.py:18
  (15 other events, 219.0 us)
Sparse Core Ops, SparseCore 0:
  13.6 41.2 all-reduce.20
  66.4 33.8 all-reduce.22
  119.6 36.4 all-reduce.24
  174.3 33.6 all-reduce.26
  228.1 36.4 all-reduce.28
  282.8 33.6 all-reduce.30
  335.8 36.4 all-reduce.32
  391.7 33.6 all-reduce.34
  446.2 36.4 all-reduce.36
  500.9 33.6 all-reduce.38
where the time goes:
time: 559 us; the launch traced here: 557 us
  waiting for transfers between devices  294 us (53%)
  blocking collectives  123 us (22%)
  matrix products  67.6 us (12%)
  other arithmetic  30.8 us (6%)
  starting transfers between devices  25.8 us (5%)
  between operations  14.8 us (3%)
    psum x5, waiting for transfers between devices, backward_sum(): lax.psum(jnp.dot(rounded, green_matrix, preferred_element_type=jnp.float3...  160 us
    psum x5, waiting for transfers between devices, forward(): return lax.psum(partial_value, 'par')  121 us
    psum x5, blocking collectives, curvatures(): image_sq = lax.psum(local_image, 'pix')  58.5 us
    dot_general x5, matrix products, forward(): lax.dot_general(rounded, green_matrix, (((1,), (1,)), ((), ())), preferre...  36.2 us
    psum x4, blocking collectives, curvatures(): smooth_sq = lax.psum(local_smooth, 'par')  33.2 us
    dot_general x5, matrix products, backward_sum(): jnp.dot(rounded, green_matrix, preferred_element_type=jnp.float32)  31.5 us
    psum x5, blocking collectives, column_squares(): return lax.psum(jnp.sum(gradient * gradient, axis=1), 'par')  31.1 us
    ppermute x9, starting transfers between devices, padded_2(): lax.ppermute(lax.slice_in_dim(block, block.shape[dim] - width, None, axis...  13.5 us
  transfers between devices with their start and end apart: 28, of which 14 were waited for; matrix products, arithmetic and copies ran while one was open for 8% of the time, Pallas kernels for 0%

commit v1 on v0

--- a/solution.py
+++ b/solution.py
@@ -5,6 +5,12 @@
 
 GRID = 128
 ITERS = 5
+
+
+def gather_and_add(x, mesh_axis):
+    shards = lax.all_gather(x, mesh_axis, axis=0, tiled=False)
+    result = shards.sum(axis=0)
+    return result
 
 
 def padded_2(block, sides, width):
@@ -36,7 +42,7 @@
     partial_value = lax.dot_general(
         rounded, green_matrix, (((1,), (1,)), ((), ())), preferred_element_type=jnp.float32
     )
-    return lax.psum(partial_value, "par")
+    return gather_and_add(partial_value, "par")
 
 
 def curvatures(image, smoothed):

time: 559 us -> 465 us (0.83)
  waiting for transfers between devices: 294 us -> 173 us
  blocking collectives: 123 us -> 147 us
  starting transfers between devices: 25.8 us -> 32.1 us
    psum x5 -> x0, waiting for transfers between devices: 121 us -> none  [forward(): return lax.psum(partial_value, 'par')]
    all_gather x0 -> x5, blocking collectives: none -> 39.5 us  [gather_and_add(): shards = lax.all_gather(x, mesh_axis, axis=0, tiled=False)]
    psum x4, blocking collectives: 33.2 us -> 25.7 us  [curvatures(): smooth_sq = lax.psum(local_smooth, 'par')]
    ppermute x9, starting transfers between devices: 13.5 us -> 20.3 us  [padded_2(): lax.ppermute(lax.slice_in_dim(block, block.shape[dim] - width, None, axis...]
  transfers between devices with their start and end apart: 28 -> 23, of which waited for: 14 -> 9; matrix products, arithmetic and copies ran while one was open for 8% -> 1% of each run, Pallas kernels for 0% -> 0%
where the time goes in v1:
time: 465 us; the launch traced here: 464 us
  waiting for transfers between devices  173 us (37%)
  blocking collectives  147 us (32%)
  matrix products  64.1 us (14%)
  starting transfers between devices  32.1 us (7%)
  other arithmetic  29.3 us (6%)
  between operations  14.5 us (3%)
    psum x5, waiting for transfers between devices, backward_sum(): lax.psum(jnp.dot(rounded, green_matrix, preferred_element_type=jnp.float3...  160 us
    psum x5, blocking collectives, curvatures(): image_sq = lax.psum(local_image, 'pix')  53.2 us
    all_gather x5, blocking collectives, gather_and_add(): shards = lax.all_gather(x, mesh_axis, axis=0, tiled=False)  39.5 us
    dot_general x5, matrix products, forward(): lax.dot_general(rounded, green_matrix, (((1,), (1,)), ((), ())), preferre...  32.9 us
    dot_general x5, matrix products, backward_sum(): jnp.dot(rounded, green_matrix, preferred_element_type=jnp.float32)  31.3 us
    psum x5, blocking collectives, column_squares(): return lax.psum(jnp.sum(gradient * gradient, axis=1), 'par')  29.1 us
    psum x4, blocking collectives, curvatures(): smooth_sq = lax.psum(local_smooth, 'par')  25.7 us
    ppermute x9, starting transfers between devices, padded_2(): lax.ppermute(lax.slice_in_dim(block, block.shape[dim] - width, None, axis...  20.3 us
  transfers between devices with their start and end apart: 23, of which 9 were waited for; matrix products, arithmetic and copies ran while one was open for 1% of the time, Pallas kernels for 0%

profile of v1, /device:TPU:0, one launch (start us, length us, event | category | flops | bytes accessed | tf_op | source)
XLA Modules:
  0.0 463.9 jit_solution(11283802326458597638)
XLA Ops:
  13.5 41.3 %all-reduce.16.cloned.1.call-done = f32[32,4096]{1,0:T(8,128)} async-done(((f32[32,4096]{1,0:T(8,128)}), f32[32,4096]{1,0:T(8,128)}) %all-reduce.16.cloned.1.call-update) | async-done | bytes 524304 | tf_op jit(solution)/shard_map/psum | solution.py:57
  56.2 6.6 %fusion.54 = f32[32,1152]{1,0:T(8,128)S(1)} fusion(bf16[32,4096]{1,0:T(8,128)(2,1)S(1)} %get-tuple-element.45, bf16[1152,4096]{1,0:T(8,128)(2,1)} %param.2), kind=kOutput, calls=%fused_computation.151 | convolution fusion | flops 301989888 | bytes 9846784 | tf_op jit(solution)/shard_map/dot_general | solution.py:42
  62.8 7.5 %all-gather = f32[128,1152]{1,0:T(8,128)S(1)} all-gather(f32[32,1152]{1,0:T(8,128)S(1)} %fusion.54), channel_id=2, replica_groups=mesh['parts'=2,'pix'=4,'par'=4] {'par'}, dimensions={0}, use_global_device_ids=true | all-gather | bytes 737280 | tf_op jit(solution)/shard_map/all_gather | solution.py:11
  74.2 10.6 %psum.142 = f32[32]{0:T(128)S(1)} all-reduce(f32[32]{0:T(128)S(1)} %multiply_reduce_fusion.13), channel_id=1, replica_groups=mesh['parts'=2,'pix'=4,'par'=4] {'pix'}, use_global_device_ids=true, to_apply=%region_5.6 | all-reduce | flops 32 | bytes 256 | tf_op jit(solution)/shard_map/psum | solution.py:51
  106.4 29.7 %all-reduce.18.cloned.1.call-done = f32[32,4096]{1,0:T(8,128)} async-done(((f32[32,4096]{1,0:T(8,128)}), f32[32,4096]{1,0:T(8,128)}) %all-reduce.18.cloned.1.call-update) | async-done | bytes 524304 | tf_op jit(solution)/shard_map/psum | solution.py:57
  143.7 6.6 %fusion.55 = f32[32,1152]{1,0:T(8,128)S(1)} fusion(bf16[32,4096]{1,0:T(8,128)(2,1)S(1)} %get-tuple-element.20, bf16[1152,4096]{1,0:T(8,128)(2,1)} %param.2), kind=kOutput, calls=%fused_computation.152 | convolution fusion | flops 301989888 | bytes 9846784 | tf_op jit(solution)/shard_map/dot_general | solution.py:42
  150.3 7.8 %all-gather.1 = f32[128,1152]{1,0:T(8,128)S(1)} all-gather(f32[32,1152]{1,0:T(8,128)S(1)} %fusion.55), channel_id=3, replica_groups=mesh['parts'=2,'pix'=4,'par'=4] {'par'}, dimensions={0}, use_global_device_ids=true | all-gather | bytes 737280 | tf_op jit(solution)/shard_map/all_gather | solution.py:11
  162.0 10.8 %psum.146 = f32[32]{0:T(128)S(1)} all-reduce(f32[32]{0:T(128)S(1)} %multiply_reduce_fusion.12), channel_id=1, replica_groups=mesh['parts'=2,'pix'=4,'par'=4] {'pix'}, use_global_device_ids=true, to_apply=%region_13.14 | all-reduce | flops 32 | bytes 256 | tf_op jit(solution)/shard_map/psum | solution.py:51
  173.9 6.4 %psum.147 = f32[32]{0:T(128)S(1)} all-reduce(f32[32]{0:T(128)S(1)} %get-tuple-element.18), channel_id=1, replica_groups=mesh['parts'=2,'pix'=4,'par'=4] {'par'}, use_global_device_ids=true, to_apply=%region_15.16 | all-reduce | flops 32 | bytes 256 | tf_op jit(solution)/shard_map/psum | solution.py:52
  194.6 29.7 %all-reduce.20.cloned.1.call-done = f32[32,4096]{1,0:T(8,128)} async-done(((f32[32,4096]{1,0:T(8,128)}), f32[32,4096]{1,0:T(8,128)}) %all-reduce.20.cloned.1.call-update) | async-done | bytes 524304 | tf_op jit(solution)/shard_map/psum | solution.py:57
  232.4 6.6 %fusion.56 = f32[32,1152]{1,0:T(8,128)S(1)} fusion(bf16[32,4096]{1,0:T(8,128)(2,1)S(1)} %get-tuple-element.14, bf16[1152,4096]{1,0:T(8,128)(2,1)} %param.2), kind=kOutput, calls=%fused_computation.153 | convolution fusion | flops 301989888 | bytes 9846784 | tf_op jit(solution)/shard_map/dot_general | solution.py:42
  239.0 8.2 %all-gather.2 = f32[128,1152]{1,0:T(8,128)} all-gather(f32[32,1152]{1,0:T(8,128)S(1)} %fusion.56), channel_id=4, replica_groups=mesh['parts'=2,'pix'=4,'par'=4] {'par'}, dimensions={0}, use_global_device_ids=true | all-gather | bytes 737280 | tf_op jit(solution)/shard_map/all_gather | solution.py:11
  252.2 10.6 %psum.150 = f32[32]{0:T(128)S(1)} all-reduce(f32[32]{0:T(128)S(1)} %multiply_reduce_fusion.11), channel_id=1, replica_groups=mesh['parts'=2,'pix'=4,'par'=4] {'pix'}, use_global_device_ids=true, to_apply=%region_21.22 | all-reduce | flops 32 | bytes 256 | tf_op jit(solution)/shard_map/psum | solution.py:51
  263.9 6.4 %psum.151 = f32[32]{0:T(128)S(1)} all-reduce(f32[32]{0:T(128)S(1)} %get-tuple-element.12), channel_id=1, replica_groups=mesh['parts'=2,'pix'=4,'par'=4] {'par'}, use_global_device_ids=true, to_apply=%region_23.24 | all-reduce | flops 32 | bytes 256 | tf_op jit(solution)/shard_map/psum | solution.py:52
  284.6 29.7 %all-reduce.22.cloned.1.call-done = f32[32,4096]{1,0:T(8,128)} async-done(((f32[32,4096]{1,0:T(8,128)}), f32[32,4096]{1,0:T(8,128)}) %all-reduce.22.cloned.1.call-update) | async-done | bytes 524304 | tf_op jit(solution)/shard_map/psum | solution.py:57
  323.1 6.6 %fusion.57 = f32[32,1152]{1,0:T(8,128)S(1)} fusion(bf16[32,4096]{1,0:T(8,128)(2,1)S(1)} %get-tuple-element.8, bf16[1152,4096]{1,0:T(8,128)(2,1)} %param.2), kind=kOutput, calls=%fused_computation.154 | convolution fusion | flops 301989888 | bytes 9846784 | tf_op jit(solution)/shard_map/dot_general | solution.py:42
  329.8 7.8 %all-gather.3 = f32[128,1152]{1,0:T(8,128)S(1)} all-gather(f32[32,1152]{1,0:T(8,128)S(1)} %fusion.57), channel_id=5, replica_groups=mesh['parts'=2,'pix'=4,'par'=4] {'par'}, dimensions={0}, use_global_device_ids=true | all-gather | bytes 737280 | tf_op jit(solution)/shard_map/all_gather | solution.py:11
  343.1 10.6 %psum.154 = f32[32]{0:T(128)S(1)} all-reduce(f32[32]{0:T(128)S(1)} %multiply_reduce_fusion.10), channel_id=1, replica_groups=mesh['parts'=2,'pix'=4,'par'=4] {'pix'}, use_global_device_ids=true, to_apply=%region_29.30 | all-reduce | flops 32 | bytes 256 | tf_op jit(solution)/shard_map/psum | solution.py:51
  355.5 6.4 %psum.155 = f32[32]{0:T(128)S(1)} all-reduce(f32[32]{0:T(128)S(1)} %get-tuple-element.6), channel_id=1, replica_groups=mesh['parts'=2,'pix'=4,'par'=4] {'par'}, use_global_device_ids=true, to_apply=%region_31.32 | all-reduce | flops 32 | bytes 256 | tf_op jit(solution)/shard_map/psum | solution.py:52
  378.3 29.8 %all-reduce.24.cloned.1.call-done = f32[32,4096]{1,0:T(8,128)} async-done(((f32[32,4096]{1,0:T(8,128)}), f32[32,4096]{1,0:T(8,128)}) %all-reduce.24.cloned.1.call-update) | async-done | bytes 524304 | tf_op jit(solution)/shard_map/psum | solution.py:57
  416.3 6.6 %fusion.58 = f32[32,1152]{1,0:T(8,128)S(1)} fusion(bf16[32,4096]{1,0:T(8,128)(2,1)S(1)} %fusion.26, bf16[1152,4096]{1,0:T(8,128)(2,1)} %param.2), kind=kOutput, calls=%fused_computation.155 | convolution fusion | flops 301989888 | bytes 9846784 | tf_op jit(solution)/shard_map/dot_general | solution.py:42
  422.8 8.2 %all-gather.4 = f32[128,1152]{1,0:T(8,128)} all-gather(f32[32,1152]{1,0:T(8,128)S(1)} %fusion.58), channel_id=6, replica_groups=mesh['parts'=2,'pix'=4,'par'=4] {'par'}, dimensions={0}, use_global_device_ids=true | all-gather | bytes 737280 | tf_op jit(solution)/shard_map/all_gather | solution.py:11
  436.0 10.6 %psum.158 = f32[32]{0:T(128)S(1)} all-reduce(f32[32]{0:T(128)S(1)} %multiply_reduce_fusion.9), channel_id=1, replica_groups=mesh['parts'=2,'pix'=4,'par'=4] {'pix'}, use_global_device_ids=true, to_apply=%region_37.38 | all-reduce | flops 32 | bytes 256 | tf_op jit(solution)/shard_map/psum | solution.py:51
  447.8 6.4 %psum.159 = f32[32]{0:T(128)S(1)} all-reduce(f32[32]{0:T(128)S(1)} %fusion.4), channel_id=1, replica_groups=mesh['parts'=2,'pix'=4,'par'=4] {'par'}, use_global_device_ids=true, to_apply=%region_39.40 | all-reduce | flops 32 | bytes 256 | tf_op jit(solution)/shard_map/psum | solution.py:52
  (185 shorter events, 137.9 us)
Async XLA Ops:
  7.2 47.7 %all-reduce.16.cloned.1.call-start = ((), (), s32[]{:S(2)}) async-start(), calls=%async_computation | async-start | bytes 1048576 | tf_op jit(solution)/shard_map/psum | solution.py:57
  13.5 122.7 %all-reduce.18.cloned.1.call-start = ((), (), s32[]{:S(2)}) async-start(), calls=%async_computation.1 | async-start | bytes 1048576 | tf_op jit(solution)/shard_map/psum | solution.py:57
  70.5 14.3 %collective-permute-start.1 = (f32[32,1,128]{2,1,0:T(1,128)S(1)}, f32[32,1,128]{2,1,0:T(1,128)S(1)}, u32[]{:S(2)}, u32[]{:S(2)}) collective-permute-start(f32[32,1,128]{2,1,0:T(1,128)S(1)} %get-tuple-element.42), channel_id=1, source_target_pairs={{0,1},{1,2},{2,3},{4,5},{5,6},{6,7},{8,9},{9,10},{10,11},{12,13},{... | collective-permute-start | bytes 49160 | tf_op jit(solution)/shard_map/ppermute | solution.py:21
  72.7 12.1 %collective-permute-start = (f32[32,1,128]{2,1,0:T(1,128)S(1)}, f32[32,1,128]{2,1,0:T(1,128)S(1)}, u32[]{:S(2)}, u32[]{:S(2)}) collective-permute-start(f32[32,1,128]{2,1,0:T(1,128)S(1)} %get-tuple-element.43), channel_id=1, source_target_pairs={{1,0},{2,1},{3,2},{5,4},{6,5},{7,6},{9,8},{10,9},{11,10},{13,12},{... | collective-permute-start | bytes 49160 | tf_op jit(solution)/shard_map/ppermute | solution.py:24
  98.4 125.9 %all-reduce.20.cloned.1.call-start = ((), (), s32[]{:S(2)}) async-start(), calls=%async_computation.2 | async-start | bytes 1048576 | tf_op jit(solution)/shard_map/psum | solution.py:57
  98.6 3.6 collective-permute-start.3
  100.9 4.6 collective-permute-start.2
  158.3 14.5 %collective-permute-start.5 = (f32[32,1,128]{2,1,0:T(1,128)S(1)}, f32[32,1,128]{2,1,0:T(1,128)S(1)}, u32[]{:S(2)}, u32[]{:S(2)}) collective-permute-start(f32[32,1,128]{2,1,0:T(1,128)S(1)} %get-tuple-element.38), channel_id=1, source_target_pairs={{0,1},{1,2},{2,3},{4,5},{5,6},{6,7},{8,9},{9,10},{10,11},{12,13},{... | collective-permute-start | bytes 49160 | tf_op jit(solution)/shard_map/ppermute | solution.py:21
  160.5 12.2 %collective-permute-start.4 = (f32[32,1,128]{2,1,0:T(1,128)S(1)}, f32[32,1,128]{2,1,0:T(1,128)S(1)}, u32[]{:S(2)}, u32[]{:S(2)}) collective-permute-start(f32[32,1,128]{2,1,0:T(1,128)S(1)} %get-tuple-element.39), channel_id=1, source_target_pairs={{1,0},{2,1},{3,2},{5,4},{6,5},{7,6},{9,8},{10,9},{11,10},{13,12},{... | collective-permute-start | bytes 49160 | tf_op jit(solution)/shard_map/ppermute | solution.py:24
  186.6 127.7 %all-reduce.22.cloned.1.call-start = ((), (), s32[]{:S(2)}) async-start(), calls=%async_computation.3 | async-start | bytes 1048576 | tf_op jit(solution)/shard_map/psum | solution.py:57
  186.9 3.6 collective-permute-start.7
  189.1 4.6 collective-permute-start.6
  248.5 14.3 %collective-permute-start.9 = (f32[32,1,128]{2,1,0:T(1,128)S(1)}, f32[32,1,128]{2,1,0:T(1,128)S(1)}, u32[]{:S(2)}, u32[]{:S(2)}) collective-permute-start(f32[32,1,128]{2,1,0:T(1,128)S(1)} %get-tuple-element.34), channel_id=1, source_target_pairs={{0,1},{1,2},{2,3},{4,5},{5,6},{6,7},{8,9},{9,10},{10,11},{12,13},{... | collective-permute-start | bytes 49160 | tf_op jit(solution)/shard_map/ppermute | solution.py:21
  250.8 12.0 %collective-permute-start.8 = (f32[32,1,128]{2,1,0:T(1,128)S(1)}, f32[32,1,128]{2,1,0:T(1,128)S(1)}, u32[]{:S(2)}, u32[]{:S(2)}) collective-permute-start(f32[32,1,128]{2,1,0:T(1,128)S(1)} %get-tuple-element.35), channel_id=1, source_target_pairs={{1,0},{2,1},{3,2},{5,4},{6,5},{7,6},{9,8},{10,9},{11,10},{13,12},{... | collective-permute-start | bytes 49160 | tf_op jit(solution)/shard_map/ppermute | solution.py:24
  270.3 91.6 %copy-start.12 = (f32[32]{0:T(128)}, f32[32]{0:T(128)S(1)}, u32[]{:S(2)}) copy-start(f32[32]{0:T(128)S(1)} %get-tuple-element.11) | copy-start | bytes 388
  276.6 131.5 %all-reduce.24.cloned.1.call-start = ((), (), s32[]{:S(2)}) async-start(), calls=%async_computation.4 | async-start | bytes 1048576 | tf_op jit(solution)/shard_map/psum | solution.py:57
  276.8 3.6 collective-permute-start.11
  279.1 4.6 collective-permute-start.10
  339.4 14.3 %collective-permute-start.13 = (f32[32,1,128]{2,1,0:T(1,128)S(1)}, f32[32,1,128]{2,1,0:T(1,128)S(1)}, u32[]{:S(2)}, u32[]{:S(2)}) collective-permute-start(f32[32,1,128]{2,1,0:T(1,128)S(1)} %get-tuple-element.30), channel_id=1, source_target_pairs={{0,1},{1,2},{2,3},{4,5},{5,6},{6,7},{8,9},{9,10},{10,11},{12,13},{... | collective-permute-start | bytes 49160 | tf_op jit(solution)/shard_map/ppermute | solution.py:21
  341.7 12.0 %collective-permute-start.12 = (f32[32,1,128]{2,1,0:T(1,128)S(1)}, f32[32,1,128]{2,1,0:T(1,128)S(1)}, u32[]{:S(2)}, u32[]{:S(2)}) collective-permute-start(f32[32,1,128]{2,1,0:T(1,128)S(1)} %get-tuple-element.31), channel_id=1, source_target_pairs={{1,0},{2,1},{3,2},{5,4},{6,5},{7,6},{9,8},{10,9},{11,10},{13,12},{... | collective-permute-start | bytes 49160 | tf_op jit(solution)/shard_map/ppermute | solution.py:24
  370.6 3.6 collective-permute-start.15
  372.8 4.6 collective-permute-start.14
  432.3 14.3 %collective-permute-start.17 = (f32[32,1,128]{2,1,0:T(1,128)S(1)}, f32[32,1,128]{2,1,0:T(1,128)S(1)}, u32[]{:S(2)}, u32[]{:S(2)}) collective-permute-start(f32[32,1,128]{2,1,0:T(1,128)S(1)} %get-tuple-element.26), channel_id=1, source_target_pairs={{0,1},{1,2},{2,3},{4,5},{5,6},{6,7},{8,9},{9,10},{10,11},{12,13},{... | collective-permute-start | bytes 49160 | tf_op jit(solution)/shard_map/ppermute | solution.py:21
  434.6 12.1 %collective-permute-start.16 = (f32[32,1,128]{2,1,0:T(1,128)S(1)}, f32[32,1,128]{2,1,0:T(1,128)S(1)}, u32[]{:S(2)}, u32[]{:S(2)}) collective-permute-start(f32[32,1,128]{2,1,0:T(1,128)S(1)} %get-tuple-element.27), channel_id=1, source_target_pairs={{1,0},{2,1},{3,2},{5,4},{6,5},{7,6},{9,8},{10,9},{11,10},{13,12},{... | collective-permute-start | bytes 49160 | tf_op jit(solution)/shard_map/ppermute | solution.py:24
  (27 other events, 335.7 us)
Sparse Core Ops, SparseCore 0:
  13.6 41.2 all-reduce.15
  98.6 37.5 all-reduce.17
  186.8 37.5 all-reduce.19
  276.8 37.5 all-reduce.21
  370.5 37.5 all-reduce.23
